TPU v7x, 1024 devices: a whole 4x4x32 slice. The times are simulated.
1024 devices in a mesh: grp: 8 (over z_lo), cp: 128 (over y, x, z_hi, core).
Axes of the slice: x: 4, y: 4, z: 32 (z_hi: 4, z_lo: 8; z = z_hi * 8 + z_lo), core: 2. Of those that a mesh axis runs over, the one named last changes fastest.
Arguments:
- query_states: bfloat16 [1024, 256, 1024], P(('grp', 'cp')), may hold values from -130 to 130
- key_states: bfloat16 [1024, 256, 128], P(('grp', 'cp')), may hold values from -8 to 8
- value_states: bfloat16 [1024, 256, 128], P(('grp', 'cp')), may hold values from -6 to 6
- grad_output: bfloat16 [1024, 256, 1024], P(('grp', 'cp')), may hold values from -6 to 6
- pair_kinds: int32 [512, 7], replicated, may hold values from 0 to 3
- row_start: int32 [65536], replicated, may hold values from 0 to 65534, as said below
Outputs:
- attn_out: bfloat16 [1024, 256, 1024], P(('grp', 'cp'))
- grad_query: bfloat16 [1024, 256, 1024], P(('grp', 'cp'))
- grad_key: bfloat16 [1024, 256, 128], P(('grp', 'cp'))
- grad_value: bfloat16 [1024, 256, 128], P(('grp', 'cp'))
Inputs may be any that keep to these rules, and one draw needn't show every extreme that they name: row_start[t] lies between max(t - 768, 0) and max(t - 1, 0).
All inputs are finite; a program needn't handle non-finite values.
Results may differ from a plain program's by a relative error of at most 0.035.
Values may be sent and summed in bfloat16 or wider, within the bound.
A program may use at most 32 MiB of HBM per device.

v0:
```python
import jax
import jax.numpy as jnp
from jax import lax
from jax.sharding import PartitionSpec as P

KVH = 4
BLK = 128
REACH = 6


def passed_along(x, axis, by):
    length = lax.axis_size(axis)
    pairs = [(i, i + by) for i in range(length) if 0 <= i + by < length]
    return lax.ppermute(x, axis, pairs)


def window_mask(kinds_block, starts_block, row_first):
    window_width = (REACH + 1) * BLK
    query_pos = row_first + jnp.arange(BLK, dtype=jnp.int32)
    key_pos = row_first - REACH * BLK + jnp.arange(window_width, dtype=jnp.int32)
    kind_cols = jnp.repeat(kinds_block[::-1], BLK)
    before = key_pos[None, :] <= query_pos[:, None]
    inside = before & (key_pos[None, :] >= starts_block[:, None])
    return (
        (kind_cols == 0)[None, :]
        | (kind_cols == 1)[None, :] & before
        | (kind_cols == 2)[None, :] & inside
    )


def block_scores(query_block, key_window, allowed, score_scale):
    scores = (
        jnp.einsum("qgd,wd->gqw", query_block, key_window, preferred_element_type=jnp.float32)
        * score_scale
    )
    return jnp.where(allowed[None], scores, -jnp.inf)


def local(query_states, key_states, value_states, grad_output, pair_kinds, row_start):
    row_count = query_states.shape[1]
    head_size = key_states.shape[2]
    group_heads = query_states.shape[2] // head_size
    block_count = row_count // BLK
    reach_owners = (REACH + block_count - 1) // block_count
    window_width = (REACH + 1) * BLK
    score_scale = head_size ** (-0.5)
    owner_index = lax.axis_index(("grp", "cp")) // KVH
    key_value = jnp.stack([key_states[0], value_states[0]])
    earlier = [
        passed_along(key_value, ("grp", "cp"), KVH * distance)
        for distance in range(reach_owners, 0, -1)
    ]
    extended = jnp.concatenate(earlier + [key_value], axis=1)
    kinds_dev = lax.dynamic_slice_in_dim(pair_kinds, owner_index * block_count, block_count, 0)
    starts_dev = lax.dynamic_slice_in_dim(row_start, owner_index * row_count, row_count, 0)
    queries_dev = query_states[0].reshape(row_count, group_heads, head_size)
    grads_dev = grad_output[0].reshape(row_count, group_heads, head_size)
    window_list = []
    output_list = []
    total_list = []
    kept_list = []
    for block_index in range(block_count):
        window_low = reach_owners * row_count + block_index * BLK - REACH * BLK
        key_window = extended[0, window_low : window_low + window_width]
        value_window = extended[1, window_low : window_low + window_width]
        row_first = owner_index * row_count + block_index * BLK
        allowed = window_mask(
            kinds_dev[block_index],
            starts_dev[block_index * BLK : (block_index + 1) * BLK],
            row_first,
        )
        query_block = queries_dev[block_index * BLK : (block_index + 1) * BLK]
        scores = block_scores(query_block, key_window, allowed, score_scale)
        row_max = jnp.max(scores, axis=-1, keepdims=True)
        log_total = row_max + jnp.log(jnp.sum(jnp.exp(scores - row_max), axis=-1, keepdims=True))
        prob_full = jnp.exp(scores - log_total)
        prob_half = prob_full.astype(jnp.bfloat16)
        block_out = jnp.einsum(
            "gqw,wd->qgd", prob_half, value_window, preferred_element_type=jnp.float32
        ).astype(jnp.bfloat16)
        window_list.append((window_low, key_window, value_window, allowed, query_block))
        output_list.append(block_out)
        total_list.append(log_total)
        kept_list.append(prob_full)
    key_grad = jnp.zeros((2, (reach_owners + 1) * row_count, head_size), jnp.float32)
    qgrad_list = []
    for block_index in range(block_count):
        window_low, key_window, value_window, allowed, query_block = window_list[block_index]
        block_out = output_list[block_index]
        grad_block = grads_dev[block_index * BLK : (block_index + 1) * BLK]
        prob_full = jnp.exp(
            block_scores(query_block, key_window, allowed, score_scale) - total_list[block_index]
        )
        prob_half = prob_full.astype(jnp.bfloat16)
        row_dot = jnp.sum(
            grad_block.astype(jnp.float32) * block_out.astype(jnp.float32), axis=-1
        ).T[:, :, None]
        prob_grad = jnp.einsum(
            "qgd,wd->gqw", grad_block, value_window, preferred_element_type=jnp.float32
        )
        score_grad = (prob_full * (prob_grad - row_dot)).astype(jnp.bfloat16)
        query_grad = (
            jnp.einsum("gqw,wd->qgd", score_grad, key_window, preferred_element_type=jnp.float32)
            * score_scale
        ).astype(jnp.bfloat16)
        key_part = (
            jnp.einsum("gqw,qgd->wd", score_grad, query_block, preferred_element_type=jnp.float32)
            * score_scale
        )
        value_part = jnp.einsum(
            "gqw,qgd->wd", prob_half, grad_block, preferred_element_type=jnp.float32
        )
        key_grad = key_grad.at[:, window_low : window_low + window_width].add(
            jnp.stack([key_part, value_part])
        )
        qgrad_list.append(query_grad)
    owner_parts = [
        key_grad[
            :, (reach_owners - distance) * row_count : (reach_owners - distance + 1) * row_count
        ]
        for distance in range(reach_owners + 1)
    ]
    summed = owner_parts[0]
    for distance in range(1, reach_owners + 1):
        summed = summed + passed_along(owner_parts[distance], ("grp", "cp"), -KVH * distance)
    attn_out = jnp.concatenate(output_list, axis=0).reshape(1, row_count, group_heads * head_size)
    grad_query = jnp.concatenate(qgrad_list, axis=0).reshape(1, row_count, group_heads * head_size)
    grad_key = summed[0].astype(jnp.bfloat16)[None]
    grad_value = summed[1].astype(jnp.bfloat16)[None]
    return (attn_out, grad_query, grad_key, grad_value)


def solution(mesh):
    placed = (
        P(("grp", "cp"), None, None),
        P(("grp", "cp"), None, None),
        P(("grp", "cp"), None, None),
        P(("grp", "cp"), None, None),
        P(),
        P(),
    )
    return jax.shard_map(
        local,
        mesh=mesh,
        in_specs=placed,
        out_specs=(
            P(("grp", "cp"), None, None),
            P(("grp", "cp"), None, None),
            P(("grp", "cp"), None, None),
            P(("grp", "cp"), None, None),
        ),
        check_vma=False,
    )
```

profile of v0, /device:TPU:991, one launch (start us, length us, event | category | flops | bytes accessed | tf_op | source)
XLA Modules:
  0.0 251.7 jit_solution(14813151894190219815)
XLA Ops:
  0.6 0.9 constant_dynamic-update-slice_fusion.1
  1.5 0.9 constant_dynamic-update-slice_fusion
  2.3 11.2 %collective-permute-start.2 = (bf16[2,256,128]{2,1,0:T(8,128)(2,1)S(1)}, bf16[2,256,128]{2,1,0:T(8,128)(2,1)S(1)}, u32[]{:S(2)}, u32[]{:S(2)}) collective-permute-start(bf16[2,256,128]{2,1,0:T(8,128)(2,1)S(1)} %constant_dynamic-update-slice_fusion), channel_id=1, source_target_pairs={{0,4},{1,5},{2,6},{3,7},{4,8},{5,9},{6,10},{7,11},{8,12},{9,13},{1... | collective-permute-start | bytes 393224 | tf_op jit(solution)/shard_map/ppermute | solution.py:14
  13.5 4.0 %collective-permute-start.1 = (bf16[2,256,128]{2,1,0:T(8,128)(2,1)S(1)}, bf16[2,256,128]{2,1,0:T(8,128)(2,1)S(1)}, u32[]{:S(2)}, u32[]{:S(2)}) collective-permute-start(bf16[2,256,128]{2,1,0:T(8,128)(2,1)S(1)} %constant_dynamic-update-slice_fusion), channel_id=1, source_target_pairs={{0,8},{1,9},{2,10},{3,11},{4,12},{5,13},{6,14},{7,15},{8,16},{9,17... | collective-permute-start | bytes 393224 | tf_op jit(solution)/shard_map/ppermute | solution.py:14
  17.5 11.6 %collective-permute-start = (bf16[2,256,128]{2,1,0:T(8,128)(2,1)S(1)}, bf16[2,256,128]{2,1,0:T(8,128)(2,1)S(1)}, u32[]{:S(2)}, u32[]{:S(2)}) collective-permute-start(bf16[2,256,128]{2,1,0:T(8,128)(2,1)S(1)} %constant_dynamic-update-slice_fusion), channel_id=1, source_target_pairs={{0,12},{1,13},{2,14},{3,15},{4,16},{5,17},{6,18},{7,19},{8,20},{9,... | collective-permute-start | bytes 393224 | tf_op jit(solution)/shard_map/ppermute | solution.py:14
  30.9 1.1 fusion.35
  32.3 1.1 fusion.34
  33.7 0.9 fusion.22
  34.6 0.9 fusion.19
  35.5 11.3 %collective-permute-done.2 = bf16[2,256,128]{2,1,0:T(8,128)(2,1)S(1)} collective-permute-done((bf16[2,256,128]{2,1,0:T(8,128)(2,1)S(1)}, bf16[2,256,128]{2,1,0:T(8,128)(2,1)S(1)}, u32[]{:S(2)}, u32[]{:S(2)}) %collective-permute-start.2) | collective-permute-done | bytes 131104 | tf_op jit(solution)/shard_map/ppermute | solution.py:14
  46.8 22.7 %collective-permute-done = bf16[2,256,128]{2,1,0:T(8,128)(2,1)S(1)} collective-permute-done((bf16[2,256,128]{2,1,0:T(8,128)(2,1)S(1)}, bf16[2,256,128]{2,1,0:T(8,128)(2,1)S(1)}, u32[]{:S(2)}, u32[]{:S(2)}) %collective-permute-start) | collective-permute-done | bytes 131104 | tf_op jit(solution)/shard_map/ppermute | solution.py:14
  71.0 1.0 multiply_reduce_fusion
  72.0 0.9 convolution_bitcast_fusion
  72.9 1.2 fusion.1
  76.9 1.0 multiply_reduce_fusion.1
  78.0 0.9 convolution_bitcast_fusion.2
  78.9 1.2 fusion.3
  81.1 3.0 %collective-permute-start.5 = (f32[2,256,128]{2,1,0:T(8,128)S(1)}, f32[2,256,128]{2,1,0:T(8,128)S(1)}, u32[]{:S(2)}, u32[]{:S(2)}) collective-permute-start(f32[2,256,128]{2,1,0:T(8,128)S(1)} %slice.147), channel_id=1, source_target_pairs={{12,0},{13,1},{14,2},{15,3},{16,4},{17,5},{18,6},{19,7},{20,8},{21... | collective-permute-start | bytes 786440 | tf_op jit(solution)/shard_map/ppermute | solution.py:14
  84.2 10.6 %collective-permute-start.3 = (f32[2,256,128]{2,1,0:T(8,128)S(1)}, f32[2,256,128]{2,1,0:T(8,128)S(1)}, u32[]{:S(2)}, u32[]{:S(2)}) collective-permute-start(f32[2,256,128]{2,1,0:T(8,128)S(1)} %get-tuple-element.40), channel_id=1, source_target_pairs={{4,0},{5,1},{6,2},{7,3},{8,4},{9,5},{10,6},{11,7},{12,8},{13,9},{1... | collective-permute-start | bytes 786440 | tf_op jit(solution)/shard_map/ppermute | solution.py:14
  94.8 8.3 %collective-permute-start.4 = (f32[2,256,128]{2,1,0:T(8,128)S(1)}, f32[2,256,128]{2,1,0:T(8,128)S(1)}, u32[]{:S(2)}, u32[]{:S(2)}) collective-permute-start(f32[2,256,128]{2,1,0:T(8,128)S(1)} %get-tuple-element.41), channel_id=1, source_target_pairs={{8,0},{9,1},{10,2},{11,3},{12,4},{13,5},{14,6},{15,7},{16,8},{17,9... | collective-permute-start | bytes 786440 | tf_op jit(solution)/shard_map/ppermute | solution.py:14
  104.1 1.0 copy.42
  105.3 1.0 copy.43
  106.3 104.1 %collective-permute-done.5 = f32[2,256,128]{2,1,0:T(8,128)S(1)} collective-permute-done((f32[2,256,128]{2,1,0:T(8,128)S(1)}, f32[2,256,128]{2,1,0:T(8,128)S(1)}, u32[]{:S(2)}, u32[]{:S(2)}) %collective-permute-start.5) | collective-permute-done | bytes 262176 | tf_op jit(solution)/shard_map/ppermute | solution.py:14
  210.4 40.6 %collective-permute-done.3 = f32[2,256,128]{2,1,0:T(8,128)S(1)} collective-permute-done((f32[2,256,128]{2,1,0:T(8,128)S(1)}, f32[2,256,128]{2,1,0:T(8,128)S(1)}, u32[]{:S(2)}, u32[]{:S(2)}) %collective-permute-start.3) | collective-permute-done | bytes 262176 | tf_op jit(solution)/shard_map/ppermute | solution.py:14
  (45 shorter events, 9.6 us)
Async XLA Ops:
  0.6 29.4 %copy-start = (s32[512,7]{0,1:T(8,128)S(1)}, s32[512,7]{0,1:T(8,128)}, u32[]{:S(2)}) copy-start(s32[512,7]{0,1:T(8,128)} %param.14) | copy-start | bytes 43012
  2.3 44.4 %collective-permute-start.2 = (bf16[2,256,128]{2,1,0:T(8,128)(2,1)S(1)}, bf16[2,256,128]{2,1,0:T(8,128)(2,1)S(1)}, u32[]{:S(2)}, u32[]{:S(2)}) collective-permute-start(bf16[2,256,128]{2,1,0:T(8,128)(2,1)S(1)} %constant_dynamic-update-slice_fusion), channel_id=1, source_target_pairs={{0,4},{1,5},{2,6},{3,7},{4,8},{5,9},{6,10},{7,11},{8,12},{9,13},{1... | collective-permute-start | bytes 393224 | tf_op jit(solution)/shard_map/ppermute | solution.py:14
  13.5 33.2 %collective-permute-start.1 = (bf16[2,256,128]{2,1,0:T(8,128)(2,1)S(1)}, bf16[2,256,128]{2,1,0:T(8,128)(2,1)S(1)}, u32[]{:S(2)}, u32[]{:S(2)}) collective-permute-start(bf16[2,256,128]{2,1,0:T(8,128)(2,1)S(1)} %constant_dynamic-update-slice_fusion), channel_id=1, source_target_pairs={{0,8},{1,9},{2,10},{3,11},{4,12},{5,13},{6,14},{7,15},{8,16},{9,17... | collective-permute-start | bytes 393224 | tf_op jit(solution)/shard_map/ppermute | solution.py:14
  17.5 52.0 %collective-permute-start = (bf16[2,256,128]{2,1,0:T(8,128)(2,1)S(1)}, bf16[2,256,128]{2,1,0:T(8,128)(2,1)S(1)}, u32[]{:S(2)}, u32[]{:S(2)}) collective-permute-start(bf16[2,256,128]{2,1,0:T(8,128)(2,1)S(1)} %constant_dynamic-update-slice_fusion), channel_id=1, source_target_pairs={{0,12},{1,13},{2,14},{3,15},{4,16},{5,17},{6,18},{7,19},{8,20},{9,... | collective-permute-start | bytes 393224 | tf_op jit(solution)/shard_map/ppermute | solution.py:14
  81.1 129.3 %collective-permute-start.5 = (f32[2,256,128]{2,1,0:T(8,128)S(1)}, f32[2,256,128]{2,1,0:T(8,128)S(1)}, u32[]{:S(2)}, u32[]{:S(2)}) collective-permute-start(f32[2,256,128]{2,1,0:T(8,128)S(1)} %slice.147), channel_id=1, source_target_pairs={{12,0},{13,1},{14,2},{15,3},{16,4},{17,5},{18,6},{19,7},{20,8},{21... | collective-permute-start | bytes 786440 | tf_op jit(solution)/shard_map/ppermute | solution.py:14
  84.2 166.8 %collective-permute-start.3 = (f32[2,256,128]{2,1,0:T(8,128)S(1)}, f32[2,256,128]{2,1,0:T(8,128)S(1)}, u32[]{:S(2)}, u32[]{:S(2)}) collective-permute-start(f32[2,256,128]{2,1,0:T(8,128)S(1)} %get-tuple-element.40), channel_id=1, source_target_pairs={{4,0},{5,1},{6,2},{7,3},{8,4},{9,5},{10,6},{11,7},{12,8},{13,9},{1... | collective-permute-start | bytes 786440 | tf_op jit(solution)/shard_map/ppermute | solution.py:14
  94.8 156.1 %collective-permute-start.4 = (f32[2,256,128]{2,1,0:T(8,128)S(1)}, f32[2,256,128]{2,1,0:T(8,128)S(1)}, u32[]{:S(2)}, u32[]{:S(2)}) collective-permute-start(f32[2,256,128]{2,1,0:T(8,128)S(1)} %get-tuple-element.41), channel_id=1, source_target_pairs={{8,0},{9,1},{10,2},{11,3},{12,4},{13,5},{14,6},{15,7},{16,8},{17,9... | collective-permute-start | bytes 786440 | tf_op jit(solution)/shard_map/ppermute | solution.py:14
where the time goes:
time: 252 us
  waiting for transfers between devices  179 us (71%)
  starting transfers between devices  48.8 us (19%)
  matrix products  10.4 us (4%)
  local copies, waits for them, and re-layouts  9.11 us (4%)
  other arithmetic  3.86 us (2%)
    ppermute x6, waiting for transfers between devices, passed_along(): return lax.ppermute(x, axis, pairs)  179 us
    ppermute x6, starting transfers between devices, passed_along(): return lax.ppermute(x, axis, pairs)  48.8 us
  transfers between devices with their start and end apart: 6, of which 4 were waited for; matrix products, arithmetic and copies ran while one was open for 4% of the time, Pallas kernels for 0%

commit v1 on v0

v1 whole, which is shorter than its diff:
```python
import jax
import jax.numpy as jnp
from jax import lax
from jax.experimental import pallas as pl
from jax.experimental.pallas import tpu as pltpu
from jax.sharding import PartitionSpec as P

KVH = 4
HD = 128
BLK = 128
REACH = 6
GQ = 8
ROWS = 256
PAIRS = GQ // 2
MESH = pl.DeviceIdType.MESH
FAR = 1 << 30
LOG2E = 1.4426950408889634

BACK3, BACK1, BACK2, OWN = 0, 512, 256, 768


def nt(a, b):
    return lax.dot_general(a, b, (((1,), (1,)), ((), ())), preferred_element_type=jnp.float32)


def nn(a, b):
    return lax.dot_general(a, b, (((1,), (0,)), ((), ())), preferred_element_type=jnp.float32)


def block_row(b, d):
    return (REACH + 1 + b - 1 - d) * BLK


def kernel(
    q_hbm, k_hbm, v_hbm, g_hbm, kinds_hbm, start_hbm,
    out_hbm, gq_hbm, gk_hbm, gv_hbm,
    q_ref, g_ref, keys, vals, keys_t, vals_t, bias, kinds, starts,
    prob, pgrad, prob_half, score_half, top8, dot8, acc_k, acc_v,
    part3, sum1, part2, got3, got1, got2, gotx, out_ref, gq_ref, final,
    local_sem, send_sem, recv_sem,
):
    grp, cp = lax.axis_index("grp"), lax.axis_index("cp")
    linear = grp * 128 + cp
    owner = linear // KVH
    z_hi = lax.rem(cp // 2, 4)
    side = z_hi // 2

    def along(step):
        moved = lax.rem(linear + step + 1024, 1024)
        return moved // 128, lax.rem(moved, 128)

    later, earlier = along(2 * KVH), along(-2 * KVH)
    across = (grp, cp + 4 - 8 * side)

    barrier = pltpu.get_barrier_semaphore()
    for peer in (later, earlier, across):
        pl.semaphore_signal(barrier, inc=1, device_id=peer, device_id_type=MESH)

    tile = pl.multiple_of((owner // 4) * 8, 8)
    loads = []
    for src, dst in (
        (k_hbm.at[0], keys.at[pl.ds(OWN, ROWS)]),
        (v_hbm.at[0], vals.at[pl.ds(OWN, ROWS)]),
        (q_hbm.at[0], q_ref),
        (g_hbm.at[0], g_ref),
        (kinds_hbm.at[pl.ds(tile, 8)], kinds),
        (start_hbm.at[pl.ds(tile, 8)], starts),
    ):
        copy = pltpu.make_async_copy(src, dst, local_sem.at[len(loads)])
        copy.start()
        loads.append(copy)

    def remote(index, src, dst, peer):
        return pltpu.make_async_remote_copy(
            src_ref=src, dst_ref=dst, send_sem=send_sem.at[index],
            recv_sem=recv_sem.at[index], device_id=peer, device_id_type=MESH,
        )

    def rows(ref, first):
        return ref.at[pl.ds(first, ROWS)]

    loads[0].wait()
    loads[1].wait()
    pl.semaphore_wait(barrier, 3)

    near = [remote(i, rows(ref, OWN), rows(ref, BACK2), later) for i, ref in enumerate((keys, vals))]
    cross_even = [remote(2 + i, rows(ref, OWN), rows(ref, BACK1), across) for i, ref in enumerate((keys, vals))]
    cross_odd = [remote(2 + i, rows(ref, BACK2), rows(ref, BACK1), across) for i, ref in enumerate((keys, vals))]
    onward = [remote(4 + i, rows(ref, BACK1), rows(ref, BACK3), later) for i, ref in enumerate((keys, vals))]

    @pl.when(side == 0)
    def _():
        cross_even[0].start()

    near[0].start()
    near[1].start()

    @pl.when(side == 0)
    def _():
        cross_even[1].start()

    for i in range(2):
        near[i].wait_recv()

        @pl.when(side == 1)
        def _():
            cross_odd[i].start()

    for copy in loads[2:]:
        copy.wait()

    lane = lax.broadcasted_iota(jnp.int32, (1, BLK), 1)
    sub = lax.broadcasted_iota(jnp.int32, (BLK, BLK), 0)
    for b in range(2):
        at = lax.rem(owner, 4) * 2 + b
        kind_row = kinds[pl.ds(at, 1), :]
        start_row = starts[pl.ds(at, 1), :]
        block = owner * 2 + b
        token = block * BLK + lane
        for d in range(REACH + 1):
            kind = jnp.broadcast_to(kind_row[:, d : d + 1], (1, BLK))
            low = jnp.where(kind == 2, start_row, jnp.where(kind == 3, FAR, -FAR))
            high = jnp.where(kind == 0, FAR, token)
            pos = (block - d) * BLK + sub
            bias[b, pl.ds(block_row(b, d), BLK), :] = jnp.where(
                (pos >= low) & (pos <= high), 0.0, -1e30
            ).astype(jnp.float32)

    acc_k[...] = jnp.zeros_like(acc_k)
    acc_v[...] = jnp.zeros_like(acc_v)
    scale = HD ** -0.5
    scale2 = scale * LOG2E

    def stacked(ref, b, pair):
        both = ref[pl.ds(b * BLK, BLK), pl.ds(pl.multiple_of(pair * 256, 256), 256)]
        return jnp.concatenate([both[:, :HD], both[:, HD:]], axis=0)

    def fold(x, op):
        return op(x.reshape(BLK // 8, 8, 256), axis=0)

    def masked(b, first, queries):
        mask = bias[b, pl.ds(first, BLK), :]
        return nt(keys[pl.ds(first, BLK), :], queries) * scale2 + jnp.concatenate([mask, mask], axis=1)

    def transposed(first):
        at = pl.ds(first, ROWS)
        keys_t[:, at] = keys[at, :].astype(jnp.float32).T.astype(jnp.bfloat16)
        vals_t[:, at] = vals[at, :].astype(jnp.float32).T.astype(jnp.bfloat16)

    far_rows = [[block_row(b, d) for d in range(REACH + 1) if block_row(b, d) // ROWS in (BACK1 // ROWS, BACK3 // ROWS)] for b in range(2)]
    near_rows = [[block_row(b, d) for d in range(REACH + 1) if block_row(b, d) // ROWS in (BACK2 // ROWS, OWN // ROWS)] for b in range(2)]

    def each_unit(step):
        def body(pair, carry):
            for b in range(2):
                step(b, pair, b * PAIRS + pair)
            return carry

        lax.fori_loop(0, PAIRS, body, 0)

    def early(b, pair, unit):
        queries, grads = stacked(q_ref, b, pair), stacked(g_ref, b, pair)
        top = None
        for first in near_rows[b]:
            score = masked(b, first, queries)
            prob[unit, pl.ds(first, BLK), :] = score
            part = fold(score, jnp.max)
            top = part if top is None else jnp.maximum(top, part)
            pgrad[unit, pl.ds(first, BLK), :] = nt(vals[pl.ds(first, BLK), :], grads)
        top8[unit] = top

    each_unit(early)
    transposed(BACK2)
    transposed(OWN)

    def wait_cross(i):
        cross_even[i].wait_recv()
        onward[i].start()
        onward[i].wait_recv()

    wait_cross(0)

    def add_to(acc, b, wanted, half, unit, other):
        runs = []
        for first in sorted(wanted):
            if runs and runs[-1][1] == first:
                runs[-1][1] = first + BLK
            else:
                runs.append([first, first + BLK])
        for first, end in runs:
            at = pl.ds(first, end - first)
            acc[at, :] += nn(half[unit, at, :], other)

    def softmax(b, pair, unit):
        queries = stacked(q_ref, b, pair)
        top = top8[unit]
        for first in far_rows[b]:
            score = masked(b, first, queries)
            prob[unit, pl.ds(first, BLK), :] = score
            top = jnp.maximum(top, fold(score, jnp.max))
        top = jnp.max(top, axis=0, keepdims=True)
        total = jnp.zeros((8, 256), jnp.float32)
        for first in far_rows[b] + near_rows[b]:
            value = jnp.exp2(prob[unit, pl.ds(first, BLK), :] - top)
            prob[unit, pl.ds(first, BLK), :] = value
            total = total + fold(value, jnp.sum)
        share = 1.0 / jnp.sum(total, axis=0, keepdims=True)
        for first in far_rows[b] + near_rows[b]:
            value = prob[unit, pl.ds(first, BLK), :] * share
            prob[unit, pl.ds(first, BLK), :] = value
            prob_half[unit, pl.ds(first, BLK), :] = value.astype(jnp.bfloat16)
        add_to(acc_v, b, far_rows[b], prob_half, unit, stacked(g_ref, b, pair))

    each_unit(softmax)

    def copies(i):
        return (
            remote(6 + i, part3.at[i], got3.at[i], earlier),
            remote(8 + i, sum1.at[i], got1.at[i], earlier),
            remote(10 + i, got1.at[i], gotx.at[i], across),
            remote(10 + i, sum1.at[i], gotx.at[i], across),
            remote(12 + i, part2.at[i], got2.at[i], earlier),
        )

    home = [copies(0), copies(1)]

    def send_three(i, acc, factor):
        part3[i] = (acc[pl.ds(BACK3, ROWS), :] * factor).astype(jnp.bfloat16)
        home[i][0].start()

    def send_two(i, acc, factor):
        part2[i] = (acc[pl.ds(BACK2, ROWS), :] * factor).astype(jnp.bfloat16)
        home[i][4].start()

    def send_one(i, acc, factor):
        home[i][0].wait_recv()
        sum1[i] = (acc[pl.ds(BACK1, ROWS), :] * factor + got3[i].astype(jnp.float32)).astype(jnp.bfloat16)

        @pl.when(side == 0)
        def _():
            home[i][1].start()

        @pl.when(side == 1)
        def _():
            home[i][3].start()

    def send_across(i):
        @pl.when(side == 0)
        def _():
            home[i][1].wait_recv()
            home[i][2].start()

    send_three(0, acc_v, 1.0)

    def near_values(b, pair, unit):
        add_to(acc_v, b, near_rows[b], prob_half, unit, stacked(g_ref, b, pair))

    each_unit(near_values)
    send_one(0, acc_v, 1.0)
    send_two(0, acc_v, 1.0)
    send_across(0)

    wait_cross(1)

    def far_grads(b, pair, unit):
        queries, grads = stacked(q_ref, b, pair), stacked(g_ref, b, pair)
        dots = jnp.zeros((8, 256), jnp.float32)
        for first in near_rows[b]:
            at = pl.ds(first, BLK)
            dots = dots + fold(prob[unit, at, :] * pgrad[unit, at, :], jnp.sum)
        for first in far_rows[b]:
            at = pl.ds(first, BLK)
            value = nt(vals[at, :], grads)
            pgrad[unit, at, :] = value
            dots = dots + fold(prob[unit, at, :] * value, jnp.sum)
        dots = jnp.broadcast_to(jnp.sum(dots, axis=0, keepdims=True), (8, 256))
        dot8[unit] = dots
        for first in far_rows[b]:
            at = pl.ds(first, BLK)
            score_half[unit, at, :] = (
                prob[unit, at, :] * (pgrad[unit, at, :] - dots[:1])
            ).astype(jnp.bfloat16)
        add_to(acc_k, b, far_rows[b], score_half, unit, queries)

    each_unit(far_grads)
    send_three(1, acc_k, scale)

    def near_grads(b, pair, unit):
        dots = dot8[unit][:1]
        for first in near_rows[b]:
            at = pl.ds(first, BLK)
            score_half[unit, at, :] = (
                prob[unit, at, :] * (pgrad[unit, at, :] - dots)
            ).astype(jnp.bfloat16)
        add_to(acc_k, b, near_rows[b], score_half, unit, stacked(q_ref, b, pair))

    each_unit(near_grads)
    send_one(1, acc_k, scale)
    send_two(1, acc_k, scale)
    transposed(BACK1)
    transposed(BACK3)
    send_across(1)

    def outputs(b, pair, unit):
        window = pl.ds(block_row(b, REACH), (REACH + 1) * BLK)
        for ref, wide, half, factor in (
            (out_ref, vals_t, prob_half, None),
            (gq_ref, keys_t, score_half, scale),
        ):
            value = nn(wide[:, window], half[unit, window, :])
            if factor is not None:
                value = value * factor
            value = value.T.astype(jnp.bfloat16)
            for h in range(2):
                columns = pl.ds(pl.multiple_of(pair * 256 + h * HD, HD), HD)
                ref[pl.ds(b * BLK, BLK), columns] = value[h * BLK : (h + 1) * BLK, :]

    each_unit(outputs)
    stores = [
        pltpu.make_async_copy(out_ref, out_hbm.at[0], local_sem.at[6]),
        pltpu.make_async_copy(gq_ref, gq_hbm.at[0], local_sem.at[7]),
    ]
    for copy in stores:
        copy.start()

    for i, acc, factor, target in ((0, acc_v, 1.0, gv_hbm), (1, acc_k, scale, gk_hbm)):
        home[i][4].wait_recv()
        home[i][2].wait_recv()
        final[i] = (
            acc[pl.ds(OWN, ROWS), :] * factor
            + got2[i].astype(jnp.float32)
            + gotx[i].astype(jnp.float32)
        ).astype(jnp.bfloat16)
        copy = pltpu.make_async_copy(final.at[i], target.at[0], local_sem.at[8 + i])
        copy.start()
        stores.append(copy)

    for copy in near + cross_even + onward:
        copy.wait_send()
    for i in range(2):
        home[i][0].wait_send()
        home[i][2].wait_send()
        home[i][4].wait_send()

        @pl.when(side == 0)
        def _():
            home[i][1].wait_send()

    for copy in stores:
        copy.wait()


def local(query_states, key_states, value_states, grad_output, pair_kinds, row_start):
    half, full = jnp.bfloat16, jnp.float32
    window = 4 * ROWS
    units = 2 * PAIRS
    moved = pltpu.VMEM((2, ROWS, HD), half)
    hbm = pl.BlockSpec(memory_space=pl.ANY)
    return pl.pallas_call(
        kernel,
        out_shape=tuple(
            jax.ShapeDtypeStruct(x.shape, half)
            for x in (query_states, query_states, key_states, key_states)
        ),
        in_specs=[hbm] * 6,
        out_specs=(hbm,) * 4,
        scratch_shapes=[
            pltpu.VMEM((ROWS, GQ * HD), half),
            pltpu.VMEM((ROWS, GQ * HD), half),
            pltpu.VMEM((window, HD), half),
            pltpu.VMEM((window, HD), half),
            pltpu.VMEM((HD, window), half),
            pltpu.VMEM((HD, window), half),
            pltpu.VMEM((2, window, BLK), full),
            pltpu.VMEM((8, REACH + 1), jnp.int32),
            pltpu.VMEM((8, BLK), jnp.int32),
            pltpu.VMEM((units, window, 256), full),
            pltpu.VMEM((units, window, 256), full),
            pltpu.VMEM((units, window, 256), half),
            pltpu.VMEM((units, window, 256), half),
            pltpu.VMEM((units, 8, 256), full),
            pltpu.VMEM((units, 8, 256), full),
            pltpu.VMEM((window, HD), full),
            pltpu.VMEM((window, HD), full),
            moved, moved, moved, moved, moved, moved, moved,
            pltpu.VMEM((ROWS, GQ * HD), half),
            pltpu.VMEM((ROWS, GQ * HD), half),
            moved,
            pltpu.SemaphoreType.DMA((10,)),
            pltpu.SemaphoreType.DMA((14,)),
            pltpu.SemaphoreType.DMA((14,)),
        ],
        compiler_params=pltpu.CompilerParams(
            collective_id=0, has_side_effects=True, vmem_limit_bytes=56 << 20
        ),
        name="exchange",
    )(query_states, key_states, value_states, grad_output, pair_kinds, row_start.reshape(-1, BLK))


def solution(mesh):
    split = P(("grp", "cp"), None, None)
    return jax.shard_map(
        local,
        mesh=mesh,
        in_specs=(split, split, split, split, P(), P()),
        out_specs=(split, split, split, split),
        check_vma=False,
    )
```

time: 252 us -> 113 us (0.45)
  the two profiles are of different devices: /device:TPU:991 before, /device:TPU:764 now
where the time goes in v1:
time: 113 us
  Pallas kernels  107 us (95%)
  local copies, waits for them, and re-layouts  5.85 us (5%)
    pallas_call x1, Pallas kernels, local(): pl.pallas_call(kernel, out_shape=tuple((jax.ShapeDtypeStruct(x.shape, hal...  107 us
    unnamed x11, local copies, waits for them, and re-layouts  5.85 us

profile of v1, /device:TPU:764, one launch (start us, length us, event | category | flops | bytes accessed | tf_op | source)
XLA Modules:
  0.0 113.1 jit_solution(2683342553728706717)
XLA Ops:
  0.6 1.6 %copy.10.kinds_hbm = s32[512,7]{1,0:T(8,128)} copy(s32[512,7]{0,1:T(8,128)} %param.10) | data formatting | bytes 28672 | tf_op args[4]
  2.2 106.6 %exchange.1 = (bf16[1,256,1024]{2,1,0:T(8,128)(2,1)}, bf16[1,256,1024]{2,1,0:T(8,128)(2,1)}, bf16[1,256,128]{2,1,0:T(8,128)(2,1)}, bf16[1,256,128]{2,1,0:T(8,128)(2,1)}) custom-call(bf16[1,256,1024]{2,1,0:T(8,128)(2,1)} %q_hbm.1, bf16[1,256,128]{2,1,0:T(8,128)(2,1)} %k_hbm.1, bf16[1,256,128]{2,1,0:T(8,128)(2,1)} %v_hbm.1, bf16[1,256,1024]{2,1,0:T(8,128)(2,1)} %g_hbm.1, ...), custom_call_target="tpu_custom_call" | custom-call | tf_op jit(solution)/shard_map/exchange/pallas_call | solution.py:359
  108.8 0.0 copy-start
  108.8 1.9 %copy.15 = bf16[1,256,1024]{2,1,0:T(8,128)(2,1)} copy(bf16[1,256,1024]{2,1,0:T(8,128)(2,1)} %get-tuple-element.8) | data formatting | bytes 1048576
  110.7 0.0 copy-done
  110.7 0.0 copy-start.2
  110.7 0.8 copy.16
  111.5 0.1 copy-done.2
  111.6 0.0 copy-start.1
  111.6 0.6 copy.17
  112.2 0.2 copy-done.1
  112.5 0.6 copy.18
Async XLA Ops:
  108.8 1.9 %copy-start = (bf16[1,256,1024]{2,1,0:T(8,128)(2,1)S(1)}, bf16[1,256,1024]{2,1,0:T(8,128)(2,1)}, u32[]{:S(2)}) copy-start(bf16[1,256,1024]{2,1,0:T(8,128)(2,1)} %get-tuple-element.9) | copy-start | bytes 1572868
  110.7 0.9 copy-start.2
  111.6 0.9 copy-start.1
